TPU v7x, 128 devices: a whole 4x4x4 slice. The times are simulated.
128 devices in a mesh: book: 8 (over y, core), path: 16 (over z, x).
Axes of the slice: x: 4, y: 4, z: 4, core: 2. Of those that a mesh axis runs over, the one named last changes fastest.
Arguments:
- states: float32 [10, 20, 262144], P(None, None, ('book', 'path')), parts along dimension 2, may hold values from -7.5 to 7.5
- itm_flags: int32 [10, 262144], P(None, ('book', 'path')), parts along dimension 1, may hold values 0 or 1
- terminal: float32 [262144], P(('book', 'path')), parts along dimension 0, may hold values from -3.5 to 5.5
- strike: float32 [8], P('book'), parts along dimension 0, may hold values from 0.025 to 0.035
- date_index: int32 [262144], P(('book', 'path')), parts along dimension 0, may hold values from 0 to 9
Outputs:
- cash_flow: float32 [262144], P(('book', 'path')), parts along dimension 0
- book_price: float32 [8], P('book'), parts along dimension 0
- coefficients: float32 [80, 231], P('book'), parts along dimension 0
There are 8 independent parts, one for each index of `book`. A program takes and returns all parts, laid end to end along the dimension named above; each array names one. Nothing has to cross between parts.
All inputs are finite; a program needn't handle non-finite values. No bound on the sum of `itm_flags` on one device may be relied on, other than what follows from the above.
Results may differ from a plain program's by a relative error of at most 0.0003.
Values sent between devices are 32-bit elements; how exact they have to be, the bound alone decides.
A program may use at most 192 MiB of HBM per device.

v0:
```python
import jax
import jax.numpy as jnp
import numpy as np
from jax import lax
from jax.sharding import Mesh
from jax.sharding import PartitionSpec as P

PATH = ("path_0", "path_1")
BOOK_PATH = ("book", "path_0", "path_1")
ridge_weight = 0.05
temper_scale = 0.5
highest = lax.Precision.HIGHEST


def one_axis_at_a_time(shard, axes):
    for axis in axes:
        shard = lax.psum(shard, axis)
    return shard


def sent_to_all(shard, axis):
    length = lax.axis_size(axis)
    return lax.all_to_all(
        jnp.broadcast_to(shard[None], (length, *shard.shape)), axis, 0, 0, tiled=True
    )


def over_copies(shard, axis):
    return sent_to_all(shard, axis).sum(axis=0)


def swap_terms(factors, strike_level):
    forwards = 0.03 * jnp.exp(0.25 * factors)
    discount = jnp.cumprod(1.0 / (1.0 + 0.25 * forwards), axis=0)
    annuity = 0.25 * jnp.sum(discount, axis=0)
    swap_rate = (1.0 - discount[-1]) / annuity
    return (100.0 * annuity * (swap_rate - strike_level), discount[0])


def basis_of(scaled, pair_left, pair_right):
    ones_row = jnp.ones((1, scaled.shape[1]), jnp.float32)
    return jnp.concatenate([ones_row, scaled, scaled[pair_left] * scaled[pair_right]], axis=0)


def gram_only(basis_rows, money_flags):
    weighted = basis_rows * money_flags
    return lax.dot_general(
        weighted,
        basis_rows,
        (((1,), (1,)), ((), ())),
        precision=highest,
        preferred_element_type=jnp.float32,
    )


def system_of(gram_sums, path_count):
    return gram_sums / path_count + ridge_weight * jnp.eye(gram_sums.shape[0], dtype=jnp.float32)


def shards(states, itm_flags, terminal, strike, date_index):
    date_count, factor_count, local_paths = states.shape
    pair_left, pair_right = np.triu_indices(factor_count)
    total_paths = local_paths * lax.axis_size(PATH)
    value_now = terminal
    coef_list = []
    money_all = itm_flags.astype(jnp.float32)
    count_all, first_all, second_all = (
        one_axis_at_a_time(jnp.sum(money_all, axis=1), PATH),
        one_axis_at_a_time(jnp.sum(money_all[:, None, :] * states, axis=2), PATH),
        one_axis_at_a_time(jnp.sum(money_all[:, None, :] * states * states, axis=2), PATH),
    )
    mean_all = first_all / count_all[:, None]
    scale_all = jnp.sqrt(second_all / count_all[:, None] - mean_all * mean_all + 1e-05)
    local_list = []
    for date_step in range(date_count):
        scaled = (states[date_step] - mean_all[date_step][:, None]) / scale_all[date_step][:, None]
        local_list.append(gram_only(basis_of(scaled, pair_left, pair_right), money_all[date_step]))
    gram_stack = lax.psum(jnp.stack(local_list, axis=0), PATH)
    chol_list = [
        jnp.linalg.cholesky(system_of(gram_stack[date_step], count_all[date_step]))
        for date_step in range(date_count)
    ]
    for date_step in range(date_count - 1, -1, -1):
        factors = states[date_step]
        exercise, discount = swap_terms(factors, strike[0])
        value_now = value_now * discount
        money_flags = money_all[date_step]
        scaled = (factors - mean_all[date_step][:, None]) / scale_all[date_step][:, None]
        basis_rows = basis_of(scaled, pair_left, pair_right)
        rhs_local = jnp.dot(
            basis_rows * money_flags,
            value_now,
            precision=highest,
            preferred_element_type=jnp.float32,
        )
        rhs_total = over_copies(rhs_local, PATH)
        coef_vector = jax.scipy.linalg.cho_solve(
            (chol_list[date_step], True), rhs_total / count_all[date_step]
        )
        continuation = jnp.dot(
            coef_vector, basis_rows, precision=highest, preferred_element_type=jnp.float32
        )
        open_date = (date_index <= date_step).astype(jnp.float32)
        weights = jax.nn.sigmoid((exercise - continuation) / temper_scale) * money_flags * open_date
        value_now = value_now + weights * (exercise - value_now)
        coef_list.append(coef_vector)
    book_sum = one_axis_at_a_time(jnp.sum(value_now), PATH)
    book_price = jnp.reshape(book_sum / total_paths, (1,))
    return (value_now, book_price, jnp.stack(coef_list[::-1], axis=0))


def solution(mesh):
    split = Mesh(mesh.devices.reshape(mesh.shape["book"], 4, 4), ("book", "path_0", "path_1"))
    return jax.shard_map(
        shards,
        mesh=split,
        in_specs=(
            P(None, None, BOOK_PATH),
            P(None, BOOK_PATH),
            P(BOOK_PATH),
            P("book"),
            P(BOOK_PATH),
        ),
        out_specs=(P(BOOK_PATH), P("book"), P("book", None)),
        check_vma=False,
    )
```

profile of v0, /device:TPU:0, one launch (start us, length us, event | category | flops | bytes accessed | tf_op | source)
XLA Modules:
  0.0 1114.3 jit_solution(1723377565558352581)
XLA Ops:
  11.3 18.4 %all-reduce.4 = (f32[10,20]{1,0:T(8,128)S(1)}, f32[10]{0:T(128)S(1)}, f32[10,20]{1,0:T(8,128)S(1)}) all-reduce(f32[10,20]{1,0:T(8,128)S(1)} %get-tuple-element.80, f32[10]{0:T(128)S(1)} %convert_reduce_fusion, f32[10,20]{1,0:T(8,128)S(1)} %get-tuple-element.79), channel_id=1, replica_groups=mesh['book'=8,'path_0'=4,'path_1'=4] {'path_0'}, use_global_device_ids=true, to_apply=%region_9.0 | all-reduce | flops 410 | bytes 3280 | tf_op jit(solution)/shard_map/psum | solution.py:17
  29.7 17.0 %all-reduce.3 = (f32[10,20]{1,0:T(8,128)S(1)}, f32[10]{0:T(128)S(1)}, f32[10,20]{1,0:T(8,128)S(1)}) all-reduce(f32[10,20]{1,0:T(8,128)S(1)} %get-tuple-element.84, f32[10]{0:T(128)S(1)} %get-tuple-element.85, f32[10,20]{1,0:T(8,128)S(1)} %get-tuple-element.86), channel_id=1, replica_groups=mesh['book'=8,'path_0'=4,'path_1'=4] {'path_1'}, use_global_device_ids=true, to_apply=%region_10.11 | all-reduce | flops 410 | bytes 3280 | tf_op jit(solution)/shard_map/psum | solution.py:17
  184.8 69.2 %all-reduce.7.cloned.1.call-done = f32[10,231,231]{1,2,0:T(8,128)} async-done(((f32[10,231,231]{1,2,0:T(8,128)}), f32[10,231,231]{1,2,0:T(8,128)}) %all-reduce.7.cloned.1.call-update) | async-done | bytes 2134456 | tf_op jit(solution)/shard_map/psum | solution.py:78
  257.5 11.7 %cholesky.504 = f32[128,128]{1,0:T(8,128)S(1)} custom-call(f32[128,128]{1,0:T(8,128)S(1)} %cholesky.880), custom_call_target="Cholesky" | custom-call | tf_op jit(solution)/shard_map/jit(cholesky)/cholesky | solution.py:80
  269.9 9.8 custom-call.31
  280.2 9.4 cholesky.524
  292.9 8.2 select_add_fusion
  304.6 12.1 %cholesky.846 = f32[128,128]{1,0:T(8,128)S(1)} custom-call(f32[128,128]{1,0:T(8,128)S(1)} %cholesky.907), custom_call_target="Cholesky" | custom-call | tf_op jit(solution)/shard_map/jit(cholesky)/cholesky | solution.py:80
  318.1 9.8 custom-call.49
  330.7 9.4 cholesky.866
  348.6 12.7 %cholesky.808 = f32[128,128]{1,0:T(8,128)S(1)} custom-call(f32[128,128]{1,0:T(8,128)} %cholesky.904), custom_call_target="Cholesky" | custom-call | tf_op jit(solution)/shard_map/jit(cholesky)/cholesky | solution.py:80
  363.2 10.6 custom-call.47
  377.2 10.2 cholesky.828
  396.5 12.5 %cholesky.770 = f32[128,128]{1,0:T(8,128)S(1)} custom-call(f32[128,128]{1,0:T(8,128)} %cholesky.901), custom_call_target="Cholesky" | custom-call | tf_op jit(solution)/shard_map/jit(cholesky)/cholesky | solution.py:80
  411.1 10.6 custom-call.45
  425.3 10.2 cholesky.790
  442.9 11.7 %cholesky.732 = f32[128,128]{1,0:T(8,128)S(1)} custom-call(f32[128,128]{1,0:T(8,128)S(1)} %cholesky.898), custom_call_target="Cholesky" | custom-call | tf_op jit(solution)/shard_map/jit(cholesky)/cholesky | solution.py:80
  456.0 9.8 custom-call.43
  468.6 9.4 cholesky.752
  484.1 11.7 %cholesky.694 = f32[128,128]{1,0:T(8,128)S(1)} custom-call(f32[128,128]{1,0:T(8,128)S(1)} %cholesky.895), custom_call_target="Cholesky" | custom-call | tf_op jit(solution)/shard_map/jit(cholesky)/cholesky | solution.py:80
  497.2 9.8 custom-call.41
  509.8 9.4 cholesky.714
  523.6 11.9 %cholesky.656 = f32[128,128]{1,0:T(8,128)S(1)} custom-call(f32[128,128]{1,0:T(8,128)S(1)} %cholesky.892), custom_call_target="Cholesky" | custom-call | tf_op jit(solution)/shard_map/jit(cholesky)/cholesky | solution.py:80
  536.9 9.8 custom-call.39
  547.8 9.4 cholesky.676
  561.8 11.7 %cholesky.618 = f32[128,128]{1,0:T(8,128)S(1)} custom-call(f32[128,128]{1,0:T(8,128)S(1)} %cholesky.889), custom_call_target="Cholesky" | custom-call | tf_op jit(solution)/shard_map/jit(cholesky)/cholesky | solution.py:80
  574.8 10.2 custom-call.37
  586.2 9.4 cholesky.638
  600.0 11.7 %cholesky.580 = f32[128,128]{1,0:T(8,128)S(1)} custom-call(f32[128,128]{1,0:T(8,128)S(1)} %cholesky.886), custom_call_target="Cholesky" | custom-call | tf_op jit(solution)/shard_map/jit(cholesky)/cholesky | solution.py:80
  613.1 9.8 custom-call.35
  624.0 9.6 cholesky.600
  638.1 11.7 %cholesky.542 = f32[128,128]{1,0:T(8,128)S(1)} custom-call(f32[128,128]{1,0:T(8,128)S(1)} %cholesky.883), custom_call_target="Cholesky" | custom-call | tf_op jit(solution)/shard_map/jit(cholesky)/cholesky | solution.py:80
  651.2 9.8 custom-call.33
  662.1 9.4 cholesky.562
  676.6 19.7 %custom-call.32 = f32[2,128,128]{1,2,0:T(8,128)S(1)} custom-call(f32[2,128,128]{2,1,0:T(8,128)S(1)} %pad_maximum_fusion.10), custom_call_target="InvertDiagBlocksLowerTriangular" | custom-call | tf_op jit(solution)/shard_map/jit(_cho_solve)/triangular_solve | solution.py:97
  719.7 21.1 %custom-call.50 = f32[2,128,128]{1,2,0:T(8,128)} custom-call(f32[2,128,128]{2,1,0:T(8,128)} %pad_maximum_fusion.19), custom_call_target="InvertDiagBlocksLowerTriangular" | custom-call | tf_op jit(solution)/shard_map/jit(_cho_solve)/triangular_solve | solution.py:97
  740.8 21.1 %custom-call.36 = f32[2,128,128]{1,2,0:T(8,128)} custom-call(f32[2,128,128]{2,1,0:T(8,128)} %pad_maximum_fusion.12), custom_call_target="InvertDiagBlocksLowerTriangular" | custom-call | tf_op jit(solution)/shard_map/jit(_cho_solve)/triangular_solve | solution.py:97
  761.9 21.1 %custom-call.38 = f32[2,128,128]{1,2,0:T(8,128)} custom-call(f32[2,128,128]{2,1,0:T(8,128)} %pad_maximum_fusion.13), custom_call_target="InvertDiagBlocksLowerTriangular" | custom-call | tf_op jit(solution)/shard_map/jit(_cho_solve)/triangular_solve | solution.py:97
  783.0 21.1 %custom-call.40 = f32[2,128,128]{1,2,0:T(8,128)} custom-call(f32[2,128,128]{2,1,0:T(8,128)} %pad_maximum_fusion.14), custom_call_target="InvertDiagBlocksLowerTriangular" | custom-call | tf_op jit(solution)/shard_map/jit(_cho_solve)/triangular_solve | solution.py:97
  804.1 21.1 %custom-call.42 = f32[2,128,128]{1,2,0:T(8,128)} custom-call(f32[2,128,128]{2,1,0:T(8,128)} %pad_maximum_fusion.15), custom_call_target="InvertDiagBlocksLowerTriangular" | custom-call | tf_op jit(solution)/shard_map/jit(_cho_solve)/triangular_solve | solution.py:97
  825.2 21.3 %custom-call.44 = f32[2,128,128]{1,2,0:T(8,128)} custom-call(f32[2,128,128]{2,1,0:T(8,128)} %pad_maximum_fusion.16), custom_call_target="InvertDiagBlocksLowerTriangular" | custom-call | tf_op jit(solution)/shard_map/jit(_cho_solve)/triangular_solve | solution.py:97
  846.5 21.1 %custom-call.46 = f32[2,128,128]{1,2,0:T(8,128)} custom-call(f32[2,128,128]{2,1,0:T(8,128)} %pad_maximum_fusion.17), custom_call_target="InvertDiagBlocksLowerTriangular" | custom-call | tf_op jit(solution)/shard_map/jit(_cho_solve)/triangular_solve | solution.py:97
  867.6 21.1 %custom-call.48 = f32[2,128,128]{1,2,0:T(8,128)} custom-call(f32[2,128,128]{2,1,0:T(8,128)} %pad_maximum_fusion.18), custom_call_target="InvertDiagBlocksLowerTriangular" | custom-call | tf_op jit(solution)/shard_map/jit(_cho_solve)/triangular_solve | solution.py:97
  888.7 21.1 %custom-call.34 = f32[2,128,128]{1,2,0:T(8,128)} custom-call(f32[2,128,128]{2,1,0:T(8,128)} %pad_maximum_fusion.11), custom_call_target="InvertDiagBlocksLowerTriangular" | custom-call | tf_op jit(solution)/shard_map/jit(_cho_solve)/triangular_solve | solution.py:97
  924.3 7.5 all-to-all-start.2
  973.9 7.5 all-to-all-done.4
  1085.2 9.5 psum.70
  1094.7 9.5 psum.71
  (668 shorter events, 410.3 us)
Async XLA Ops:
  7.2 39.6 %copy-start.142 = (s32[210]{0:T(256)S(1)}, s32[210]{0:T(256)}, u32[]{:S(2)}) copy-start(s32[210]{0:T(256)} %constant.243) | copy-start | bytes 2524
  7.2 39.6 %copy-start.143 = (s32[210]{0:T(256)S(1)}, s32[210]{0:T(256)}, u32[]{:S(2)}) copy-start(s32[210]{0:T(256)} %constant.242) | copy-start | bytes 2524
  9.2 117.4 %copy-start.71 = (f32[1,2048]{1,0:T(1,128)}, f32[1,2048]{1,0:T(1,128)S(1)}, u32[]{:S(2)}) copy-start(f32[1,2048]{1,0:T(1,128)S(1)} %get-tuple-element.145) | copy-start | bytes 24580
  9.2 126.6 %copy-start.75 = (f32[1,2048]{1,0:T(1,128)}, f32[1,2048]{1,0:T(1,128)S(1)}, u32[]{:S(2)}) copy-start(f32[1,2048]{1,0:T(1,128)S(1)} %get-tuple-element.144) | copy-start | bytes 24580
  9.2 129.3 %copy-start.77 = (f32[1,2048]{1,0:T(1,128)}, f32[1,2048]{1,0:T(1,128)S(1)}, u32[]{:S(2)}) copy-start(f32[1,2048]{1,0:T(1,128)S(1)} %get-tuple-element.143) | copy-start | bytes 24580
  9.2 132.0 %copy-start.79 = (f32[1,2048]{1,0:T(1,128)}, f32[1,2048]{1,0:T(1,128)S(1)}, u32[]{:S(2)}) copy-start(f32[1,2048]{1,0:T(1,128)S(1)} %get-tuple-element.142) | copy-start | bytes 24580
  9.3 134.7 %copy-start.81 = (f32[1,2048]{1,0:T(1,128)}, f32[1,2048]{1,0:T(1,128)S(1)}, u32[]{:S(2)}) copy-start(f32[1,2048]{1,0:T(1,128)S(1)} %get-tuple-element.141) | copy-start | bytes 24580
  9.3 137.6 %copy-start.83 = (f32[1,2048]{1,0:T(1,128)}, f32[1,2048]{1,0:T(1,128)S(1)}, u32[]{:S(2)}) copy-start(f32[1,2048]{1,0:T(1,128)S(1)} %get-tuple-element.140) | copy-start | bytes 24580
  9.3 140.3 %copy-start.85 = (f32[1,2048]{1,0:T(1,128)}, f32[1,2048]{1,0:T(1,128)S(1)}, u32[]{:S(2)}) copy-start(f32[1,2048]{1,0:T(1,128)S(1)} %get-tuple-element.139) | copy-start | bytes 24580
  9.3 143.0 %copy-start.88 = (f32[1,2048]{1,0:T(1,128)}, f32[1,2048]{1,0:T(1,128)S(1)}, u32[]{:S(2)}) copy-start(f32[1,2048]{1,0:T(1,128)S(1)} %get-tuple-element.138) | copy-start | bytes 24580
  9.3 145.7 %copy-start.90 = (f32[1,2048]{1,0:T(1,128)}, f32[1,2048]{1,0:T(1,128)S(1)}, u32[]{:S(2)}) copy-start(f32[1,2048]{1,0:T(1,128)S(1)} %get-tuple-element.137) | copy-start | bytes 24580
  9.3 148.4 %copy-start.96 = (f32[1,2048]{1,0:T(1,128)}, f32[1,2048]{1,0:T(1,128)S(1)}, u32[]{:S(2)}) copy-start(f32[1,2048]{1,0:T(1,128)S(1)} %get-tuple-element.146) | copy-start | bytes 24580
  60.6 97.1 %copy-start.127 = (f32[1,2048]{1,0:T(1,128)}, f32[1,2048]{1,0:T(1,128)S(1)}, u32[]{:S(2)}) copy-start(f32[1,2048]{1,0:T(1,128)S(1)} %broadcast.242) | copy-start | bytes 24580
  62.9 121.1 %all-to-all-start = ((f32[16,1,231]{2,1,0:T(1,128)}), f32[16,1,231]{2,1,0:T(1,128)S(1)}, u32[]{:S(2)}, u32[]{:S(2)}) async-start(f32[16,1,231]{2,1,0:T(1,128)} %broadcast_in_dim.208), calls=%async_computation | async-start | bytes 32768 | tf_op jit(solution)/shard_map/all_to_all | solution.py:23
  66.7 187.3 %all-reduce.7.cloned.1.call-start = ((), (), s32[]{:S(2)}) async-start(), calls=%async_computation.10 | async-start | bytes 4751360 | tf_op jit(solution)/shard_map/psum | solution.py:78
  115.8 36.5 %copy-start.30 = (f32[210,2048]{1,0:T(8,128)}, f32[210,2048]{1,0:T(8,128)S(1)}, u32[]{:S(2)}) copy-start(f32[210,2048]{1,0:T(8,128)S(1)} %mul.603) | copy-start | bytes 5160964
  118.4 25.6 %copy-start.24 = (f32[210,2048]{1,0:T(8,128)}, f32[210,2048]{1,0:T(8,128)S(1)}, u32[]{:S(2)}) copy-start(f32[210,2048]{1,0:T(8,128)S(1)} %mul.591) | copy-start | bytes 5160964
  132.9 22.1 %copy-start.32 = (f32[210,2048]{1,0:T(8,128)}, f32[210,2048]{1,0:T(8,128)S(1)}, u32[]{:S(2)}) copy-start(f32[210,2048]{1,0:T(8,128)S(1)} %mul.607) | copy-start | bytes 5160964
  634.2 42.3 %copy-start.52 = (f32[128,25]{1,0:T(8,128)S(1)}, f32[128,25]{1,0:T(8,128)}, u32[]{:S(2)}) copy-start(f32[128,25]{1,0:T(8,128)} %pad_convert_fusion) | copy-start | bytes 38404
  634.2 42.3 %copy-start.61 = (f32[103,103]{1,0:T(8,128)S(1)}, f32[103,103]{1,0:T(8,128)}, u32[]{:S(2)}) copy-start(f32[103,103]{1,0:T(8,128)} %triangular_solve.700) | copy-start | bytes 127312
  636.2 40.4 %copy-start.60 = (f32[1,128,128]{2,1,0:T(8,128)S(1)}, f32[1,128,128]{2,1,0:T(8,128)}, u32[]{:S(2)}) copy-start(f32[1,128,128]{2,1,0:T(8,128)} %slice_bitcast_fusion.19) | copy-start | bytes 196612
  637.9 61.2 %copy-start.128 = (f32[1,2048]{1,0:T(1,128)S(1)}, f32[1,2048]{1,0:T(1,128)}, u32[]{:S(2)}) copy-start(f32[1,2048]{1,0:T(1,128)} %copy-done.127) | copy-start | bytes 24580
  672.8 29.0 %copy-start.46 = (s32[2048]{0:T(1024)S(1)}, s32[2048]{0:T(1024)}, u32[]{:S(2)}) copy-start(s32[2048]{0:T(1024)} %param.54) | copy-start | bytes 24580
  672.8 29.0 %copy-start.97 = (f32[1,2048]{1,0:T(1,128)S(1)}, f32[1,2048]{1,0:T(1,128)}, u32[]{:S(2)}) copy-start(f32[1,2048]{1,0:T(1,128)} %copy-done.96) | copy-start | bytes 24580
  672.8 29.0 %copy-start.101 = (f32[2048]{0:T(1024)S(1)}, f32[2048]{0:T(1024)}, u32[]{:S(2)}) copy-start(f32[2048]{0:T(1024)} %copy-done.100) | copy-start | bytes 24580
  672.8 29.1 %copy-start.118 = (f32[1,2048]{1,0:T(1,128)S(1)}, f32[1,2048]{1,0:T(1,128)}, u32[]{:S(2)}) copy-start(f32[1,2048]{1,0:T(1,128)} %get-tuple-element.135) | copy-start | bytes 24580
  672.8 29.1 %copy-start.121 = (f32[1,2048]{1,0:T(1,128)S(1)}, f32[1,2048]{1,0:T(1,128)}, u32[]{:S(2)}) copy-start(f32[1,2048]{1,0:T(1,128)} %get-tuple-element.134) | copy-start | bytes 24580
  674.2 27.7 %copy-start.91 = (f32[1,2048]{1,0:T(1,128)S(1)}, f32[1,2048]{1,0:T(1,128)}, u32[]{:S(2)}) copy-start(f32[1,2048]{1,0:T(1,128)} %copy-done.90) | copy-start | bytes 24580
  704.3 205.5 %all-to-all-start.1 = ((f32[16,1,231]{2,1,0:T(1,128)}), f32[16,1,231]{2,1,0:T(1,128)}, u32[]{:S(2)}, u32[]{:S(2)}) async-start(f32[16,1,231]{2,1,0:T(1,128)} %broadcast_in_dim.211), calls=%async_computation.1 | async-start | bytes 32768 | tf_op jit(solution)/shard_map/all_to_all | solution.py:23
  713.0 208.9 %copy-start.31 = (f32[210,2048]{1,0:T(8,128)S(1)}, f32[210,2048]{1,0:T(8,128)}, u32[]{:S(2)}) copy-start(f32[210,2048]{1,0:T(8,128)} %copy-done.30) | copy-start | bytes 5160964
  713.0 208.9 %copy-start.89 = (f32[1,2048]{1,0:T(1,128)S(1)}, f32[1,2048]{1,0:T(1,128)}, u32[]{:S(2)}) copy-start(f32[1,2048]{1,0:T(1,128)} %copy-done.88) | copy-start | bytes 24580
  923.6 24.9 %copy-start.102 = (f32[2048]{0:T(1024)S(1)}, f32[2048]{0:T(1024)}, u32[]{:S(2)}) copy-start(f32[2048]{0:T(1024)} %reduce_sum.223) | copy-start | bytes 24580
  923.6 24.9 %copy-start.116 = (f32[1,2048]{1,0:T(1,128)S(1)}, f32[1,2048]{1,0:T(1,128)}, u32[]{:S(2)}) copy-start(f32[1,2048]{1,0:T(1,128)} %get-tuple-element.130) | copy-start | bytes 24580
  923.7 24.9 %copy-start.117 = (f32[1,2048]{1,0:T(1,128)S(1)}, f32[1,2048]{1,0:T(1,128)}, u32[]{:S(2)}) copy-start(f32[1,2048]{1,0:T(1,128)} %get-tuple-element.131) | copy-start | bytes 24580
  923.7 24.9 %copy-start.125 = (f32[2048]{0:T(1024)S(1)}, f32[2048]{0:T(1024)}, u32[]{:S(2)}) copy-start(f32[2048]{0:T(1024)} %copy-done.124) | copy-start | bytes 24580
  923.7 24.9 %copy-start.29 = (f32[210,2048]{1,0:T(8,128)S(1)}, f32[210,2048]{1,0:T(8,128)}, u32[]{:S(2)}) copy-start(f32[210,2048]{1,0:T(8,128)} %copy-done.28) | copy-start | bytes 5160964
  923.7 24.9 %copy-start.86 = (f32[1,2048]{1,0:T(1,128)S(1)}, f32[1,2048]{1,0:T(1,128)}, u32[]{:S(2)}) copy-start(f32[1,2048]{1,0:T(1,128)} %copy-done.85) | copy-start | bytes 24580
  923.7 24.9 %copy-start.130 = (f32[1,2048]{1,0:T(1,128)S(1)}, f32[1,2048]{1,0:T(1,128)}, u32[]{:S(2)}) copy-start(f32[1,2048]{1,0:T(1,128)} %copy-done.127) | copy-start | bytes 24580
  924.3 14.9 %all-to-all-start.2 = ((f32[16,1,231]{2,1,0:T(1,128)}), f32[16,1,231]{2,1,0:T(1,128)S(1)}, u32[]{:S(2)}, u32[]{:S(2)}) async-start(f32[16,1,231]{2,1,0:T(1,128)} %broadcast_in_dim.214), calls=%async_computation.2 | async-start | bytes 32768 | tf_op jit(solution)/shard_map/all_to_all | solution.py:23
  951.0 11.0 all-to-all-start.3
  970.4 11.0 all-to-all-start.4
  990.0 11.4 %all-to-all-start.5 = ((f32[16,1,231]{2,1,0:T(1,128)}), f32[16,1,231]{2,1,0:T(1,128)S(1)}, u32[]{:S(2)}, u32[]{:S(2)}) async-start(f32[16,1,231]{2,1,0:T(1,128)} %broadcast_in_dim.223), calls=%async_computation.5 | async-start | bytes 32768 | tf_op jit(solution)/shard_map/all_to_all | solution.py:23
  1009.8 11.0 all-to-all-start.6
  1029.3 11.0 all-to-all-start.7
  1048.7 11.2 %all-to-all-start.8 = ((f32[16,1,231]{2,1,0:T(1,128)}), f32[16,1,231]{2,1,0:T(1,128)S(1)}, u32[]{:S(2)}, u32[]{:S(2)}) async-start(f32[16,1,231]{2,1,0:T(1,128)} %broadcast_in_dim.232), calls=%async_computation.8 | async-start | bytes 32768 | tf_op jit(solution)/shard_map/all_to_all | solution.py:23
  1067.7 37.1 %copy-start.136 = (f32[1,231]{1,0:T(1,128)S(1)}, f32[1,231]{1,0:T(1,128)}, u32[]{:S(2)}) copy-start(f32[1,231]{1,0:T(1,128)} %fusion.420) | copy-start | bytes 2776
  1067.8 37.1 %copy-start.137 = (f32[1,231]{1,0:T(1,128)S(1)}, f32[1,231]{1,0:T(1,128)}, u32[]{:S(2)}) copy-start(f32[1,231]{1,0:T(1,128)} %fusion.419) | copy-start | bytes 2776
  1068.4 11.0 all-to-all-start.9
  (107 other events, 1008.8 us)
Sparse Core Ops, SparseCore 0:
  160.6 93.2 all-reduce.6
where the time goes:
time: 1120 us; the launch traced here: 1110 us
  other arithmetic  630 us (56%)
  waiting for transfers between devices  127 us (11%)
  matrix products  123 us (11%)
  local copies, waits for them, and re-layouts  106 us (9%)
  blocking collectives  54.3 us (5%)
  starting transfers between devices  41.8 us (4%)
  between operations  31.9 us (3%)
    another operation x70, other arithmetic, shards(): jnp.linalg.cholesky(system_of(gram_stack[date_step], count_all[date_step]))  336 us
    another operation x34, other arithmetic, shards(): jax.scipy.linalg.cho_solve((chol_list[date_step], True), rhs_total / coun...  229 us
    psum x1, waiting for transfers between devices, shards(): gram_stack = lax.psum(jnp.stack(local_list, axis=0), PATH)  69.2 us
    all_to_all x10, waiting for transfers between devices, sent_to_all(): lax.all_to_all(jnp.broadcast_to(shard[None], (length, *shard.shape)), axi...  58 us
    psum x4, blocking collectives, one_axis_at_a_time(): shard = lax.psum(shard, axis)  54.3 us
    all_to_all x10, starting transfers between devices, sent_to_all(): lax.all_to_all(jnp.broadcast_to(shard[None], (length, *shard.shape)), axi...  41.5 us
    another operation x60, matrix products, shards(): jax.scipy.linalg.cho_solve((chol_list[date_step], True), rhs_total / coun...  33.7 us
    dot_general x10, matrix products, gram_only(): lax.dot_general(weighted, basis_rows, (((1,), (1,)), ((), ())), precision...  27.3 us
  transfers between devices with their start and end apart: 11, of which 9 were waited for; matrix products, arithmetic and copies ran while one was open for 27% of the time, Pallas kernels for 0%

commit v1 on v0

--- a/solution.py
+++ b/solution.py
@@ -75,7 +75,7 @@
     for date_step in range(date_count):
         scaled = (states[date_step] - mean_all[date_step][:, None]) / scale_all[date_step][:, None]
         local_list.append(gram_only(basis_of(scaled, pair_left, pair_right), money_all[date_step]))
-    gram_stack = lax.psum(jnp.stack(local_list, axis=0), PATH)
+    gram_stack = lax.psum(lax.psum(jnp.stack(local_list, axis=0), "path_0"), "path_1")
     chol_list = [
         jnp.linalg.cholesky(system_of(gram_stack[date_step], count_all[date_step]))
         for date_step in range(date_count)

time: 1120 us -> 1180 us (1.054)
  waiting for transfers between devices: 127 us -> 167 us
    psum x1 -> x2, waiting for transfers between devices: 69.2 us -> 107 us  [the longest x1 55.9 us: shards(): lax.psum(jnp.stack(local_list, axis=0), 'path_0')]
    dot_general x10, matrix products: 16.6 us -> 28.5 us  [shards(): jnp.dot(basis_rows * money_flags, value_now, precision=highest, preferred...]
    unnamed x288 -> x218, local copies, waits for them, and re-layouts: 22.9 us -> 24.1 us
  transfers between devices with their start and end apart: 11 -> 12, of which waited for: 9 -> 10; matrix products, arithmetic and copies ran while one was open for 27% -> 26% of each run, Pallas kernels for 0% -> 0%
where the time goes in v1:
time: 1180 us; the launch traced here: 1170 us
  other arithmetic  629 us (53%)
  waiting for transfers between devices  167 us (14%)
  matrix products  131 us (11%)
  local copies, waits for them, and re-layouts  109 us (9%)
  blocking collectives  54.3 us (5%)
  starting transfers between devices  42.8 us (4%)
  between operations  31.5 us (3%)
    another operation x70, other arithmetic, shards(): jnp.linalg.cholesky(system_of(gram_stack[date_step], count_all[date_step]))  336 us
    another operation x34, other arithmetic, shards(): jax.scipy.linalg.cho_solve((chol_list[date_step], True), rhs_total / coun...  231 us
    all_to_all x10, waiting for transfers between devices, sent_to_all(): lax.all_to_all(jnp.broadcast_to(shard[None], (length, *shard.shape)), axi...  60.1 us
    psum x1, waiting for transfers between devices, shards(): lax.psum(jnp.stack(local_list, axis=0), 'path_0')  55.9 us
    psum x4, blocking collectives, one_axis_at_a_time(): shard = lax.psum(shard, axis)  54.3 us
    psum x1, waiting for transfers between devices, shards(): lax.psum(lax.psum(jnp.stack(local_list, axis=0), 'path_0'), 'path_1')  51 us
    all_to_all x10, starting transfers between devices, sent_to_all(): lax.all_to_all(jnp.broadcast_to(shard[None], (length, *shard.shape)), axi...  42.2 us
    dot_general x10, matrix products, shards(): jnp.dot(basis_rows * money_flags, value_now, precision=highest, preferred...  28.5 us
  transfers between devices with their start and end apart: 12, of which 10 were waited for; matrix products, arithmetic and copies ran while one was open for 26% of the time, Pallas kernels for 0%

profile of v1, /device:TPU:0, one launch (start us, length us, event | category | flops | bytes accessed | tf_op | source)
XLA Modules:
  0.0 1165.6 jit_solution(866275226232868939)
XLA Ops:
  11.3 18.4 %all-reduce.4 = (f32[10,20]{1,0:T(8,128)S(1)}, f32[10]{0:T(128)S(1)}, f32[10,20]{1,0:T(8,128)S(1)}) all-reduce(f32[10,20]{1,0:T(8,128)S(1)} %get-tuple-element.80, f32[10]{0:T(128)S(1)} %convert_reduce_fusion, f32[10,20]{1,0:T(8,128)S(1)} %get-tuple-element.79), channel_id=1, replica_groups=mesh['book'=8,'path_0'=4,'path_1'=4] {'path_0'}, use_global_device_ids=true, to_apply=%region_9.0 | all-reduce | flops 410 | bytes 3280 | tf_op jit(solution)/shard_map/psum | solution.py:17
  29.7 17.0 %all-reduce.3 = (f32[10,20]{1,0:T(8,128)S(1)}, f32[10]{0:T(128)S(1)}, f32[10,20]{1,0:T(8,128)S(1)}) all-reduce(f32[10,20]{1,0:T(8,128)S(1)} %get-tuple-element.84, f32[10]{0:T(128)S(1)} %get-tuple-element.85, f32[10,20]{1,0:T(8,128)S(1)} %get-tuple-element.86), channel_id=1, replica_groups=mesh['book'=8,'path_0'=4,'path_1'=4] {'path_1'}, use_global_device_ids=true, to_apply=%region_10.0 | all-reduce | flops 410 | bytes 3280 | tf_op jit(solution)/shard_map/psum | solution.py:17
  170.0 55.9 %all-reduce.8.cloned.1.call-done = f32[10,231,231]{1,2,0:T(8,128)} async-done(((f32[10,231,231]{1,2,0:T(8,128)}), f32[10,231,231]{1,2,0:T(8,128)}) %all-reduce.8.cloned.1.call-update) | async-done | bytes 2134456 | tf_op jit(solution)/shard_map/psum | solution.py:78
  240.2 51.0 %all-reduce.10.cloned.1.call-done = f32[10,231,231]{1,2,0:T(8,128)} async-done(((f32[10,231,231]{1,2,0:T(8,128)}), f32[10,231,231]{1,2,0:T(8,128)}) %all-reduce.10.cloned.1.call-update) | async-done | bytes 2134456 | tf_op jit(solution)/shard_map/psum | solution.py:78
  294.7 11.7 %cholesky.504 = f32[128,128]{1,0:T(8,128)S(1)} custom-call(f32[128,128]{1,0:T(8,128)S(1)} %cholesky.880), custom_call_target="Cholesky" | custom-call | tf_op jit(solution)/shard_map/jit(cholesky)/cholesky | solution.py:80
  307.1 9.8 custom-call.31
  317.4 9.4 cholesky.524
  330.1 8.3 select_add_fusion
  342.0 12.1 %cholesky.846 = f32[128,128]{1,0:T(8,128)S(1)} custom-call(f32[128,128]{1,0:T(8,128)S(1)} %cholesky.907), custom_call_target="Cholesky" | custom-call | tf_op jit(solution)/shard_map/jit(cholesky)/cholesky | solution.py:80
  355.5 9.8 custom-call.49
  368.0 9.4 cholesky.866
  385.9 12.7 %cholesky.808 = f32[128,128]{1,0:T(8,128)S(1)} custom-call(f32[128,128]{1,0:T(8,128)} %cholesky.904), custom_call_target="Cholesky" | custom-call | tf_op jit(solution)/shard_map/jit(cholesky)/cholesky | solution.py:80
  400.6 10.6 custom-call.47
  414.6 10.2 cholesky.828
  433.8 12.5 %cholesky.770 = f32[128,128]{1,0:T(8,128)S(1)} custom-call(f32[128,128]{1,0:T(8,128)} %cholesky.901), custom_call_target="Cholesky" | custom-call | tf_op jit(solution)/shard_map/jit(cholesky)/cholesky | solution.py:80
  448.4 10.8 custom-call.45
  462.5 10.2 cholesky.790
  480.2 11.7 %cholesky.732 = f32[128,128]{1,0:T(8,128)S(1)} custom-call(f32[128,128]{1,0:T(8,128)S(1)} %cholesky.898), custom_call_target="Cholesky" | custom-call | tf_op jit(solution)/shard_map/jit(cholesky)/cholesky | solution.py:80
  493.2 9.8 custom-call.43
  505.8 9.8 cholesky.752
  521.3 11.7 %cholesky.694 = f32[128,128]{1,0:T(8,128)S(1)} custom-call(f32[128,128]{1,0:T(8,128)S(1)} %cholesky.895), custom_call_target="Cholesky" | custom-call | tf_op jit(solution)/shard_map/jit(cholesky)/cholesky | solution.py:80
  534.4 9.8 custom-call.41
  547.0 9.4 cholesky.714
  562.1 11.9 %cholesky.656 = f32[128,128]{1,0:T(8,128)S(1)} custom-call(f32[128,128]{1,0:T(8,128)S(1)} %cholesky.892), custom_call_target="Cholesky" | custom-call | tf_op jit(solution)/shard_map/jit(cholesky)/cholesky | solution.py:80
  575.3 9.8 custom-call.39
  587.9 9.4 cholesky.676
  602.9 11.7 %cholesky.618 = f32[128,128]{1,0:T(8,128)S(1)} custom-call(f32[128,128]{1,0:T(8,128)S(1)} %cholesky.889), custom_call_target="Cholesky" | custom-call | tf_op jit(solution)/shard_map/jit(cholesky)/cholesky | solution.py:80
  616.0 10.2 custom-call.37
  629.0 9.4 cholesky.638
  644.0 11.7 %cholesky.580 = f32[128,128]{1,0:T(8,128)S(1)} custom-call(f32[128,128]{1,0:T(8,128)S(1)} %cholesky.886), custom_call_target="Cholesky" | custom-call | tf_op jit(solution)/shard_map/jit(cholesky)/cholesky | solution.py:80
  657.1 9.8 custom-call.35
  669.7 9.6 cholesky.600
  685.0 11.7 %cholesky.542 = f32[128,128]{1,0:T(8,128)S(1)} custom-call(f32[128,128]{1,0:T(8,128)S(1)} %cholesky.883), custom_call_target="Cholesky" | custom-call | tf_op jit(solution)/shard_map/jit(cholesky)/cholesky | solution.py:80
  698.0 9.8 custom-call.33
  710.6 9.4 cholesky.562
  726.5 20.5 %custom-call.32 = f32[2,128,128]{1,2,0:T(8,128)S(1)} custom-call(f32[2,128,128]{2,1,0:T(8,128)} %pad_maximum_fusion.10), custom_call_target="InvertDiagBlocksLowerTriangular" | custom-call | tf_op jit(solution)/shard_map/jit(_cho_solve)/triangular_solve | solution.py:97
  774.6 20.5 %custom-call.50 = f32[2,128,128]{1,2,0:T(8,128)S(1)} custom-call(f32[2,128,128]{2,1,0:T(8,128)} %pad_maximum_fusion.19), custom_call_target="InvertDiagBlocksLowerTriangular" | custom-call | tf_op jit(solution)/shard_map/jit(_cho_solve)/triangular_solve | solution.py:97
  795.1 20.3 %custom-call.36 = f32[2,128,128]{1,2,0:T(8,128)} custom-call(f32[2,128,128]{2,1,0:T(8,128)S(1)} %pad_maximum_fusion.12), custom_call_target="InvertDiagBlocksLowerTriangular" | custom-call | tf_op jit(solution)/shard_map/jit(_cho_solve)/triangular_solve | solution.py:97
  815.3 21.1 %custom-call.38 = f32[2,128,128]{1,2,0:T(8,128)} custom-call(f32[2,128,128]{2,1,0:T(8,128)} %pad_maximum_fusion.13), custom_call_target="InvertDiagBlocksLowerTriangular" | custom-call | tf_op jit(solution)/shard_map/jit(_cho_solve)/triangular_solve | solution.py:97
  836.4 21.1 %custom-call.40 = f32[2,128,128]{1,2,0:T(8,128)} custom-call(f32[2,128,128]{2,1,0:T(8,128)} %pad_maximum_fusion.14), custom_call_target="InvertDiagBlocksLowerTriangular" | custom-call | tf_op jit(solution)/shard_map/jit(_cho_solve)/triangular_solve | solution.py:97
  857.5 21.1 %custom-call.42 = f32[2,128,128]{1,2,0:T(8,128)} custom-call(f32[2,128,128]{2,1,0:T(8,128)} %pad_maximum_fusion.15), custom_call_target="InvertDiagBlocksLowerTriangular" | custom-call | tf_op jit(solution)/shard_map/jit(_cho_solve)/triangular_solve | solution.py:97
  878.6 20.4 %custom-call.44 = f32[2,128,128]{1,2,0:T(8,128)} custom-call(f32[2,128,128]{2,1,0:T(8,128)S(1)} %pad_maximum_fusion.16), custom_call_target="InvertDiagBlocksLowerTriangular" | custom-call | tf_op jit(solution)/shard_map/jit(_cho_solve)/triangular_solve | solution.py:97
  899.1 20.5 %custom-call.46 = f32[2,128,128]{1,2,0:T(8,128)S(1)} custom-call(f32[2,128,128]{2,1,0:T(8,128)} %pad_maximum_fusion.17), custom_call_target="InvertDiagBlocksLowerTriangular" | custom-call | tf_op jit(solution)/shard_map/jit(_cho_solve)/triangular_solve | solution.py:97
  919.5 20.5 %custom-call.48 = f32[2,128,128]{1,2,0:T(8,128)S(1)} custom-call(f32[2,128,128]{2,1,0:T(8,128)} %pad_maximum_fusion.18), custom_call_target="InvertDiagBlocksLowerTriangular" | custom-call | tf_op jit(solution)/shard_map/jit(_cho_solve)/triangular_solve | solution.py:97
  940.0 21.1 %custom-call.34 = f32[2,128,128]{1,2,0:T(8,128)} custom-call(f32[2,128,128]{2,1,0:T(8,128)} %pad_maximum_fusion.11), custom_call_target="InvertDiagBlocksLowerTriangular" | custom-call | tf_op jit(solution)/shard_map/jit(_cho_solve)/triangular_solve | solution.py:97
  981.1 7.6 all-to-all-done.2
  1136.5 9.5 psum.78
  1146.0 9.5 psum.79
  (601 shorter events, 433.9 us)
Async XLA Ops:
  7.2 39.6 %copy-start.107 = (s32[210]{0:T(256)S(1)}, s32[210]{0:T(256)}, u32[]{:S(2)}) copy-start(s32[210]{0:T(256)} %constant.243) | copy-start | bytes 2524
  7.2 39.6 %copy-start.108 = (s32[210]{0:T(256)S(1)}, s32[210]{0:T(256)}, u32[]{:S(2)}) copy-start(s32[210]{0:T(256)} %constant.242) | copy-start | bytes 2524
  9.2 117.4 %copy-start.51 = (f32[1,2048]{1,0:T(1,128)}, f32[1,2048]{1,0:T(1,128)S(1)}, u32[]{:S(2)}) copy-start(f32[1,2048]{1,0:T(1,128)S(1)} %get-tuple-element.145) | copy-start | bytes 24580
  9.2 126.5 %copy-start.55 = (f32[1,2048]{1,0:T(1,128)}, f32[1,2048]{1,0:T(1,128)S(1)}, u32[]{:S(2)}) copy-start(f32[1,2048]{1,0:T(1,128)S(1)} %get-tuple-element.144) | copy-start | bytes 24580
  9.2 129.3 %copy-start.57 = (f32[1,2048]{1,0:T(1,128)}, f32[1,2048]{1,0:T(1,128)S(1)}, u32[]{:S(2)}) copy-start(f32[1,2048]{1,0:T(1,128)S(1)} %get-tuple-element.143) | copy-start | bytes 24580
  9.2 132.0 %copy-start.59 = (f32[1,2048]{1,0:T(1,128)}, f32[1,2048]{1,0:T(1,128)S(1)}, u32[]{:S(2)}) copy-start(f32[1,2048]{1,0:T(1,128)S(1)} %get-tuple-element.142) | copy-start | bytes 24580
  9.3 134.7 %copy-start.61 = (f32[1,2048]{1,0:T(1,128)}, f32[1,2048]{1,0:T(1,128)S(1)}, u32[]{:S(2)}) copy-start(f32[1,2048]{1,0:T(1,128)S(1)} %get-tuple-element.141) | copy-start | bytes 24580
  9.3 137.6 %copy-start.63 = (f32[1,2048]{1,0:T(1,128)}, f32[1,2048]{1,0:T(1,128)S(1)}, u32[]{:S(2)}) copy-start(f32[1,2048]{1,0:T(1,128)S(1)} %get-tuple-element.140) | copy-start | bytes 24580
  9.3 140.3 %copy-start.65 = (f32[1,2048]{1,0:T(1,128)}, f32[1,2048]{1,0:T(1,128)S(1)}, u32[]{:S(2)}) copy-start(f32[1,2048]{1,0:T(1,128)S(1)} %get-tuple-element.139) | copy-start | bytes 24580
  9.3 143.0 %copy-start.67 = (f32[1,2048]{1,0:T(1,128)}, f32[1,2048]{1,0:T(1,128)S(1)}, u32[]{:S(2)}) copy-start(f32[1,2048]{1,0:T(1,128)S(1)} %get-tuple-element.138) | copy-start | bytes 24580
  9.3 145.7 %copy-start.70 = (f32[1,2048]{1,0:T(1,128)}, f32[1,2048]{1,0:T(1,128)S(1)}, u32[]{:S(2)}) copy-start(f32[1,2048]{1,0:T(1,128)S(1)} %get-tuple-element.137) | copy-start | bytes 24580
  9.3 148.4 %copy-start.74 = (f32[1,2048]{1,0:T(1,128)}, f32[1,2048]{1,0:T(1,128)S(1)}, u32[]{:S(2)}) copy-start(f32[1,2048]{1,0:T(1,128)S(1)} %get-tuple-element.146) | copy-start | bytes 24580
  60.6 97.1 %copy-start.101 = (f32[1,2048]{1,0:T(1,128)}, f32[1,2048]{1,0:T(1,128)S(1)}, u32[]{:S(2)}) copy-start(f32[1,2048]{1,0:T(1,128)S(1)} %broadcast.242) | copy-start | bytes 24580
  62.9 176.6 %all-to-all-start = ((f32[16,1,231]{2,1,0:T(1,128)}), f32[16,1,231]{2,1,0:T(1,128)S(1)}, u32[]{:S(2)}, u32[]{:S(2)}) async-start(f32[16,1,231]{2,1,0:T(1,128)} %broadcast_in_dim.208), calls=%async_computation | async-start | bytes 32768 | tf_op jit(solution)/shard_map/all_to_all | solution.py:23
  66.7 159.3 %all-reduce.8.cloned.1.call-start = ((), (), s32[]{:S(2)}) async-start(), calls=%async_computation.10 | async-start | bytes 4751360 | tf_op jit(solution)/shard_map/psum | solution.py:78
  115.7 36.6 %copy-start.23 = (f32[210,2048]{1,0:T(8,128)}, f32[210,2048]{1,0:T(8,128)S(1)}, u32[]{:S(2)}) copy-start(f32[210,2048]{1,0:T(8,128)S(1)} %mul.603) | copy-start | bytes 5160964
  118.4 25.6 %copy-start.20 = (f32[210,2048]{1,0:T(8,128)}, f32[210,2048]{1,0:T(8,128)S(1)}, u32[]{:S(2)}) copy-start(f32[210,2048]{1,0:T(8,128)S(1)} %mul.591) | copy-start | bytes 5160964
  121.0 20.2 %copy-start.19 = (f32[210,2048]{1,0:T(8,128)}, f32[210,2048]{1,0:T(8,128)S(1)}, u32[]{:S(2)}) copy-start(f32[210,2048]{1,0:T(8,128)S(1)} %mul.587) | copy-start | bytes 5160964
  132.8 22.2 %copy-start.24 = (f32[210,2048]{1,0:T(8,128)}, f32[210,2048]{1,0:T(8,128)S(1)}, u32[]{:S(2)}) copy-start(f32[210,2048]{1,0:T(8,128)S(1)} %mul.607) | copy-start | bytes 5160964
  160.5 130.7 %all-reduce.10.cloned.1.call-start = ((), (), s32[]{:S(2)}) async-start(), calls=%async_computation.11 | async-start | bytes 4751360 | tf_op jit(solution)/shard_map/psum | solution.py:78
  679.9 45.0 %copy-start.43 = (f32[128,25]{1,0:T(8,128)S(1)}, f32[128,25]{1,0:T(8,128)}, u32[]{:S(2)}) copy-start(f32[128,25]{1,0:T(8,128)} %pad_convert_fusion) | copy-start | bytes 38404
  684.1 65.7 %copy-start.102 = (f32[1,2048]{1,0:T(1,128)S(1)}, f32[1,2048]{1,0:T(1,128)}, u32[]{:S(2)}) copy-start(f32[1,2048]{1,0:T(1,128)} %copy-done.101) | copy-start | bytes 24580
  685.0 40.8 %copy-start.49 = (f32[1,128,128]{2,1,0:T(8,128)S(1)}, f32[1,128,128]{2,1,0:T(8,128)}, u32[]{:S(2)}) copy-start(f32[1,128,128]{2,1,0:T(8,128)} %slice_bitcast_fusion.19) | copy-start | bytes 196612
  721.3 31.2 %copy-start.33 = (s32[2048]{0:T(1024)S(1)}, s32[2048]{0:T(1024)}, u32[]{:S(2)}) copy-start(s32[2048]{0:T(1024)} %param.54) | copy-start | bytes 24580
  721.3 31.2 %copy-start.75 = (f32[1,2048]{1,0:T(1,128)S(1)}, f32[1,2048]{1,0:T(1,128)}, u32[]{:S(2)}) copy-start(f32[1,2048]{1,0:T(1,128)} %copy-done.74) | copy-start | bytes 24580
  721.3 31.2 %copy-start.79 = (f32[2048]{0:T(1024)S(1)}, f32[2048]{0:T(1024)}, u32[]{:S(2)}) copy-start(f32[2048]{0:T(1024)} %copy-done.78) | copy-start | bytes 24580
  721.3 31.2 %copy-start.81 = (f32[2048]{0:T(1024)S(1)}, f32[2048]{0:T(1024)}, u32[]{:S(2)}) copy-start(f32[2048]{0:T(1024)} %reduce_sum.216) | copy-start | bytes 24580
  721.3 31.2 %copy-start.95 = (f32[1,2048]{1,0:T(1,128)S(1)}, f32[1,2048]{1,0:T(1,128)}, u32[]{:S(2)}) copy-start(f32[1,2048]{1,0:T(1,128)} %get-tuple-element.135) | copy-start | bytes 24580
  721.3 31.2 %copy-start.98 = (f32[1,2048]{1,0:T(1,128)S(1)}, f32[1,2048]{1,0:T(1,128)}, u32[]{:S(2)}) copy-start(f32[1,2048]{1,0:T(1,128)} %get-tuple-element.134) | copy-start | bytes 24580
  722.7 29.9 %copy-start.71 = (f32[1,2048]{1,0:T(1,128)S(1)}, f32[1,2048]{1,0:T(1,128)}, u32[]{:S(2)}) copy-start(f32[1,2048]{1,0:T(1,128)} %copy-done.70) | copy-start | bytes 24580
  754.9 206.3 %all-to-all-start.1 = ((f32[16,1,231]{2,1,0:T(1,128)}), f32[16,1,231]{2,1,0:T(1,128)S(1)}, u32[]{:S(2)}, u32[]{:S(2)}) async-start(f32[16,1,231]{2,1,0:T(1,128)} %broadcast_in_dim.211), calls=%async_computation.1 | async-start | bytes 32768 | tf_op jit(solution)/shard_map/all_to_all | solution.py:23
  768.0 201.0 %copy-start.80 = (f32[2048]{0:T(1024)S(1)}, f32[2048]{0:T(1024)}, u32[]{:S(2)}) copy-start(f32[2048]{0:T(1024)} %reduce_sum.221) | copy-start | bytes 24580
  768.0 201.0 %copy-start.97 = (f32[1,2048]{1,0:T(1,128)S(1)}, f32[1,2048]{1,0:T(1,128)}, u32[]{:S(2)}) copy-start(f32[1,2048]{1,0:T(1,128)} %get-tuple-element.132) | copy-start | bytes 24580
  768.0 201.8 %copy-start.68 = (f32[1,2048]{1,0:T(1,128)S(1)}, f32[1,2048]{1,0:T(1,128)}, u32[]{:S(2)}) copy-start(f32[1,2048]{1,0:T(1,128)} %copy-done.67) | copy-start | bytes 24580
  969.0 20.4 %copy-start.48 = (f32[2,128,128]{1,2,0:T(8,128)S(1)}, f32[2,128,128]{1,2,0:T(8,128)}, u32[]{:S(2)}) copy-start(f32[2,128,128]{1,2,0:T(8,128)} %custom-call.36) | copy-start | bytes 393220
  969.0 21.5 %copy-start.103 = (f32[1,2048]{1,0:T(1,128)S(1)}, f32[1,2048]{1,0:T(1,128)}, u32[]{:S(2)}) copy-start(f32[1,2048]{1,0:T(1,128)} %copy-done.101) | copy-start | bytes 24580
  972.9 20.2 %copy-start.94 = (f32[1,2048]{1,0:T(1,128)S(1)}, f32[1,2048]{1,0:T(1,128)}, u32[]{:S(2)}) copy-start(f32[1,2048]{1,0:T(1,128)} %get-tuple-element.130) | copy-start | bytes 24580
  972.9 20.2 %copy-start.96 = (f32[1,2048]{1,0:T(1,128)S(1)}, f32[1,2048]{1,0:T(1,128)}, u32[]{:S(2)}) copy-start(f32[1,2048]{1,0:T(1,128)} %get-tuple-element.131) | copy-start | bytes 24580
  972.9 20.2 %copy-start.66 = (f32[1,2048]{1,0:T(1,128)S(1)}, f32[1,2048]{1,0:T(1,128)}, u32[]{:S(2)}) copy-start(f32[1,2048]{1,0:T(1,128)} %copy-done.65) | copy-start | bytes 24580
  973.6 15.1 %all-to-all-start.2 = ((f32[16,1,231]{2,1,0:T(1,128)}), f32[16,1,231]{2,1,0:T(1,128)S(1)}, u32[]{:S(2)}, u32[]{:S(2)}) async-start(f32[16,1,231]{2,1,0:T(1,128)} %broadcast_in_dim.214), calls=%async_computation.2 | async-start | bytes 32768 | tf_op jit(solution)/shard_map/all_to_all | solution.py:23
  997.0 11.0 all-to-all-start.3
  1016.3 11.0 all-to-all-start.4
  1035.6 11.4 all-to-all-start.5
  1055.3 11.0 all-to-all-start.6
  1076.3 11.0 all-to-all-start.7
  1097.2 11.2 all-to-all-start.8
  1117.7 38.5 %copy-start.105 = (f32[1,231]{1,0:T(1,128)S(1)}, f32[1,231]{1,0:T(1,128)}, u32[]{:S(2)}) copy-start(f32[1,231]{1,0:T(1,128)} %fusion.420) | copy-start | bytes 2776
  1118.3 11.0 all-to-all-start.9
  (73 other events, 621.9 us)
Sparse Core Ops, SparseCore 0:
  160.6 65.2 all-reduce.7
  228.3 62.8 all-reduce.9
